TPU v7x, 32 devices: a whole 2x2x4 slice. The times are simulated.
32 devices in a mesh: dp: 16 (over z, y, x), head: 2 (over core).
Axes of the slice: x: 2, y: 2, z: 4, core: 2. Of those that a mesh axis runs over, the one named last changes fastest.
Arguments:
- tokens: bfloat16 [16384, 768], P(('dp', 'head')), may hold values from -6 to 6
- mixer_gain: float32 [768], replicated, may hold values from 0.1 to 1.9
- joined_weight: bfloat16 [768, 2304], replicated, may hold values from -0.21875 to 0.21875
- merge_weight: bfloat16 [768, 768], replicated, may hold values from -0.875 to 0.875
- feeder_gain: float32 [768], replicated, may hold values from 0.1 to 1.9
- expand_weight: bfloat16 [768, 2304], replicated, may hold values from -0.21875 to 0.21875
- shrink_weight: bfloat16 [1152, 768], replicated, may hold values from -0.1875 to 0.1875
- doc_lengths: int32 [16, 4], P('dp'), may hold values from 1 to 512, 1024 in all within a row
- padding: int32 [16], P('dp'), may hold values from 0 to 255
- cotangent: bfloat16 [16384, 768], P(('dp', 'head')), may hold values from -6 to 6
Outputs:
- block_output: bfloat16 [16384, 768], P(('dp', 'head'))
- tokens_gradient: bfloat16 [16384, 768], P(('dp', 'head'))
- mixer_gradient: float32 [768], P('head')
- joined_gradient: float32 [768, 2304], P('head')
- merge_gradient: float32 [768, 768], P('head')
- feeder_gradient: float32 [768], P('head')
- expand_gradient: float32 [768, 2304], P('head')
- shrink_gradient: float32 [1152, 768], P('head')
Inputs may be any that keep to these rules, and one draw needn't show every extreme that they name: `doc_lengths`: each slot's 4 lengths are positive, sum to 1024, and the longest is exactly 512.
All inputs are finite; a program needn't handle non-finite values.
Results may differ from a plain program's by a relative error of at most 0.013.
Values may be sent and summed in bfloat16 or wider, within the bound.
A program may use at most 192 MiB of HBM per device.

v0:
```python
import math

import jax
import jax.numpy as jnp
from jax import lax
from jax.sharding import PartitionSpec as P

HD = 64
SLOT = 1024


epsilon = 1e-05
rotary_base = 160000.0
masked_score = -1e30


def normalize(values, gain):
    centred = values - jnp.mean(values, axis=-1, keepdims=True)
    factor = lax.rsqrt(jnp.mean(centred * centred, axis=-1, keepdims=True) + epsilon)
    plain = centred * factor
    return (plain, factor, plain * gain)


def normalize_back(change, plain, factor, gain):
    scaled = change * gain
    gain_change = jnp.sum(change * plain, axis=0)
    inner = (
        scaled
        - jnp.mean(scaled, axis=-1, keepdims=True)
        - plain * jnp.mean(scaled * plain, axis=-1, keepdims=True)
    )
    return (factor * inner, gain_change)


def slot_layout(lengths_row, padding_row):
    places = jnp.arange(SLOT, dtype=jnp.int32)
    bounds = jnp.cumsum(lengths_row)
    passed = (places[:, None] >= bounds[None, :]).astype(jnp.int32)
    segment = jnp.sum(passed, axis=1)
    start = jnp.sum(passed * lengths_row[None, :], axis=1)
    position = (places - start).astype(jnp.float32)
    kept = jnp.logical_not(places >= SLOT - padding_row)
    allowed = (segment[:, None] == segment[None, :]) & kept[:, None] & kept[None, :]
    allowed = allowed | (places[:, None] == places[None, :])
    return (position, allowed)


def turning(position):
    halfway = HD // 2
    rates = jnp.exp(jnp.arange(halfway, dtype=jnp.float32) * (-2.0 * math.log(rotary_base) / HD))
    angles = position[:, None] * rates[None, :]
    doubled = jnp.concatenate([angles, angles], axis=1)
    return (jnp.cos(doubled), jnp.sin(doubled))


def rotate(values, cosine, sine):
    halfway = values.shape[-1] // 2
    turned = jnp.concatenate([-values[..., halfway:], values[..., :halfway]], axis=-1)
    return values * cosine[:, None, :] + turned * sine[:, None, :]


def unrotate(change, cosine, sine):
    halfway = change.shape[-1] // 2
    twisted = change * sine[:, None, :]
    turned = jnp.concatenate([twisted[..., halfway:], -twisted[..., :halfway]], axis=-1)
    return change * cosine[:, None, :] + turned


def gelu_slope(inner):
    normal_cdf = 0.5 * (1.0 + lax.erf(inner * (1.0 / math.sqrt(2.0))))
    density = jnp.exp(-0.5 * inner * inner) * (1.0 / math.sqrt(2.0 * math.pi))
    return normal_cdf + inner * density


def slot_scores(packed, lengths_row, padding_row):
    position, allowed = slot_layout(lengths_row, padding_row)
    cosine, sine = turning(position)
    parts = packed.reshape(SLOT, 3, packed.shape[-1] // HD, HD)
    queries = rotate(parts[:, 0].astype(jnp.float32), cosine, sine).astype(jnp.bfloat16)
    keys = rotate(parts[:, 1].astype(jnp.float32), cosine, sine).astype(jnp.bfloat16)
    scores = jnp.einsum("qhd,khd->hqk", queries, keys, preferred_element_type=jnp.float32) * HD ** (
        -0.5
    )
    scores = jnp.where(allowed[None], scores, masked_score)
    return (queries, keys, parts[:, 2], scores, cosine, sine)


def slot_forward(item):
    packed, lengths_row, padding_row = item
    queries, keys, values, scores, cosine, sine = slot_scores(packed, lengths_row, padding_row)
    top = jnp.max(scores, axis=-1, keepdims=True)
    weights = jnp.exp(scores - top)
    total = jnp.sum(weights, axis=-1, keepdims=True)
    probs = (weights / total).astype(jnp.bfloat16)
    mixed = jnp.einsum("hqk,khd->qhd", probs, values, preferred_element_type=jnp.float32)
    return (
        mixed.astype(jnp.bfloat16).reshape(SLOT, packed.shape[-1]),
        (top + jnp.log(total))[..., 0],
    )


def slot_backward(item):
    packed, change_mixed, log_total, lengths_row, padding_row = item
    queries, keys, values, scores, cosine, sine = slot_scores(packed, lengths_row, padding_row)
    share = packed.shape[-1]
    probs = jnp.exp(scores - log_total[..., None])
    change_out = change_mixed.reshape(SLOT, share // HD, HD)
    drift = jnp.einsum("qhd,khd->hqk", change_out, values, preferred_element_type=jnp.float32)
    centre = jnp.sum(probs * drift, axis=-1, keepdims=True)
    score_change = (probs * (drift - centre)).astype(jnp.bfloat16)
    value_change = jnp.einsum(
        "hqk,qhd->khd", probs.astype(jnp.bfloat16), change_out, preferred_element_type=jnp.float32
    )
    query_change = jnp.einsum(
        "hqk,khd->qhd", score_change, keys, preferred_element_type=jnp.float32
    ) * HD ** (-0.5)
    key_change = jnp.einsum(
        "hqk,qhd->khd", score_change, queries, preferred_element_type=jnp.float32
    ) * HD ** (-0.5)
    query_change = unrotate(query_change, cosine, sine)
    key_change = unrotate(key_change, cosine, sine)
    stacked = jnp.stack([query_change, key_change, value_change], axis=1)
    return stacked.astype(jnp.bfloat16).reshape(SLOT, 3, share)


def shards(
    tokens,
    mixer_gain,
    joined_weight,
    merge_weight,
    feeder_gain,
    expand_weight,
    shrink_weight,
    doc_lengths,
    padding,
    cotangent,
):
    group = lax.axis_size("head")
    rows = tokens.shape[0]
    width = tokens.shape[1]
    share = width // group
    slots = rows * group // SLOT
    hidden_width = shrink_weight.shape[0]
    inputs = tokens.astype(jnp.float32)
    plain_one, factor_one, normed_one = normalize(inputs, mixer_gain)
    first_in = normed_one.astype(jnp.bfloat16)
    joined = jnp.dot(first_in, joined_weight, preferred_element_type=jnp.float32).astype(
        jnp.bfloat16
    )
    spread = lax.all_to_all(
        joined.reshape(rows, 3, group, share), "head", split_axis=2, concat_axis=0, tiled=True
    )
    packed = spread.reshape(slots, SLOT, 3, share)
    mixed_heads, log_totals = lax.map(slot_forward, (packed, doc_lengths, padding))
    mixed_back = lax.all_to_all(
        mixed_heads.reshape(rows * group, 1, share), "head", split_axis=0, concat_axis=1, tiled=True
    )
    mixed = mixed_back.reshape(rows, width)
    residual = inputs + jnp.dot(mixed, merge_weight, preferred_element_type=jnp.float32)
    plain_two, factor_two, normed_two = normalize(residual, feeder_gain)
    second_in = normed_two.astype(jnp.bfloat16)
    expanded = jnp.dot(second_in, expand_weight, preferred_element_type=jnp.float32)
    inner = expanded[:, :hidden_width]
    gate = expanded[:, hidden_width:]
    activated = jax.nn.gelu(inner, approximate=False)
    hidden = (activated * gate).astype(jnp.bfloat16)
    block_output = (
        residual + jnp.dot(hidden, shrink_weight, preferred_element_type=jnp.float32)
    ).astype(jnp.bfloat16)
    shrink_grad = jnp.dot(hidden.T, cotangent, preferred_element_type=jnp.float32)
    hidden_change = jnp.dot(cotangent, shrink_weight.T, preferred_element_type=jnp.float32)
    expand_change = jnp.concatenate(
        [hidden_change * gate * gelu_slope(inner), hidden_change * activated], axis=1
    ).astype(jnp.bfloat16)
    expand_grad = jnp.dot(second_in.T, expand_change, preferred_element_type=jnp.float32)
    second_change = jnp.dot(expand_change, expand_weight.T, preferred_element_type=jnp.float32)
    residual_part, feeder_grad = normalize_back(second_change, plain_two, factor_two, feeder_gain)
    residual_change = cotangent.astype(jnp.float32) + residual_part
    residual_low = residual_change.astype(jnp.bfloat16)
    merge_grad = jnp.dot(mixed.T, residual_low, preferred_element_type=jnp.float32)
    mixed_change = jnp.dot(residual_low, merge_weight.T, preferred_element_type=jnp.float32).astype(
        jnp.bfloat16
    )
    change_heads = lax.all_to_all(
        mixed_change.reshape(rows, group, share), "head", split_axis=1, concat_axis=0, tiled=True
    )
    head_changes = lax.map(
        slot_backward,
        (packed, change_heads.reshape(slots, SLOT, share), log_totals, doc_lengths, padding),
    )
    returned = lax.all_to_all(
        head_changes.reshape(rows * group, 3, 1, share),
        "head",
        split_axis=0,
        concat_axis=2,
        tiled=True,
    )
    joined_change = returned.reshape(rows, 3 * width)
    joined_grad = jnp.dot(first_in.T, joined_change, preferred_element_type=jnp.float32)
    first_change = jnp.dot(joined_change, joined_weight.T, preferred_element_type=jnp.float32)
    input_part, mixer_grad = normalize_back(first_change, plain_one, factor_one, mixer_gain)
    tokens_gradient = (residual_change + input_part).astype(jnp.bfloat16)
    grad_shares = (
        lax.psum_scatter(
            mixer_grad.astype(jnp.bfloat16), "head", scatter_dimension=0, tiled=True
        ).astype(jnp.float32),
        lax.psum_scatter(
            joined_grad.astype(jnp.bfloat16), "head", scatter_dimension=0, tiled=True
        ).astype(jnp.float32),
        lax.psum_scatter(
            merge_grad.astype(jnp.bfloat16), "head", scatter_dimension=0, tiled=True
        ).astype(jnp.float32),
        lax.psum_scatter(
            feeder_grad.astype(jnp.bfloat16), "head", scatter_dimension=0, tiled=True
        ).astype(jnp.float32),
        lax.psum_scatter(
            expand_grad.astype(jnp.bfloat16), "head", scatter_dimension=0, tiled=True
        ).astype(jnp.float32),
        lax.psum_scatter(
            shrink_grad.astype(jnp.bfloat16), "head", scatter_dimension=0, tiled=True
        ).astype(jnp.float32),
    )
    mixer_total, joined_total, merge_total, feeder_total, expand_total, shrink_total = lax.psum(
        (
            grad_shares[0],
            grad_shares[1],
            grad_shares[2],
            grad_shares[3],
            grad_shares[4],
            grad_shares[5],
        ),
        "dp",
    )
    return (
        block_output,
        tokens_gradient,
        mixer_total,
        joined_total,
        merge_total,
        feeder_total,
        expand_total,
        shrink_total,
    )


def solution(mesh):
    in_specs = (
        P(("dp", "head"), None),
        P(),
        P(),
        P(),
        P(),
        P(),
        P(),
        P("dp", None),
        P("dp"),
        P(("dp", "head"), None),
    )
    out_specs = (
        P(("dp", "head"), None),
        P(("dp", "head"), None),
        P("head"),
        P("head", None),
        P("head", None),
        P("head"),
        P("head", None),
        P("head", None),
    )
    return jax.shard_map(shards, mesh=mesh, in_specs=in_specs, out_specs=out_specs, check_vma=False)
```

profile of v0, /device:TPU:0, one launch (start us, length us, event | category | flops | bytes accessed | tf_op | source)
XLA Modules:
  0.0 718.7 jit_solution(11395483345596921816)
XLA Ops:
  10.8 5.8 convolution_convert_fusion.2
  16.5 5.6 reshape.336
  22.1 3.4 copy.72
  25.5 4.9 all-to-all-start
  30.9 2.7 all-to-all-done
  33.6 6.8 copy.73
  40.4 6.6 reshape.337
  46.9 3.4 fusion.47
  53.1 2.5 slice_negate_fusion.2
  58.0 10.6 %fusion.63 = (f32[6,1024]{1,0:T(8,128)S(1)}, f32[6,1024,1024]{1,2,0:T(8,128)}) fusion(bf16[1024,6,64]{0,2,1:T(8,128)(2,1)S(1)} %get-tuple-element.67, bf16[1024,6,64]{0,2,1:T(8,128)(2,1)S(1)} %get-tuple-element.66, pred[1024,1024]{0,1:T(8,128)(4,1)S(1)} %fusion.6), kind=kOutput, calls=%fused_computation.133 | convolution fusion | flops 824174592 | bytes 27811840 | tf_op jit(solution)/shard_map/while/body/eval_jaxpr/qhd,khd->hqk/dot_general | solution.py:81
  68.6 10.2 %fusion = f32[6,1024]{1,0:T(8,128)S(1)} fusion(f32[6,1024,1024]{1,2,0:T(8,128)} %get-tuple-element.87, f32[6,1024]{1,0:T(8,128)S(1)} %get-tuple-element.86), kind=kLoop, calls=%fused_computation.6 | loop fusion | flops 12576768 | bytes 25214976 | tf_op jit(solution)/shard_map/while/body/eval_jaxpr/reduce_sum | solution.py:93
  78.9 11.4 %fusion.46 = bf16[6,64,1024]{2,1,0:T(8,128)(2,1)} fusion(f32[6,1024,1024]{1,2,0:T(8,128)} %get-tuple-element.87, f32[6,1024]{1,0:T(8,128)S(1)} %fusion, f32[6,1024]{1,0:T(8,128)S(1)} %get-tuple-element.86, bf16[1024,3,6,64]{0,3,2,1:T(8,128)(2,1)S(1)} %copy-done.3), kind=kOutput, calls=%fused_computation.88 | convolution fusion | flops 824573952 | bytes 26804224 | tf_op jit(solution)/shard_map/while/body/eval_jaxpr/hqk,khd->qhd/dot_general | solution.py:95
  90.8 3.0 reduce
  93.8 2.3 copy.95
  96.1 2.0 reshape.349
  98.1 6.5 all_to_all.60
  104.6 2.6 reshape.350
  107.2 2.4 copy.91
  109.6 2.3 copy.76
  111.9 2.6 fusion.64
  114.9 2.1 fusion.59
  117.0 8.2 %multiply_convert_fusion.1 = (bf16[512,1152]{1,0:T(8,128)(2,1)S(1)}, f32[512,1152]{1,0:T(8,128)}, bf16[512,1152]{1,0:T(8,128)(2,1)S(1)}) fusion(f32[512,2304]{1,0:T(8,128)S(1)} %fusion.59, bf16[512,768]{1,0:T(8,128)(2,1)S(1)} %copy-done.16, bf16[1152,768]{1,0:T(8,128)(2,1)S(1)} %copy-done.27), kind=kOutput, calls=%fused_computation.32 | convolution fusion | flops 951386112 | bytes 11993088 | tf_op jit(solution)/shard_map/dot_general | solution.py:171
  125.2 2.3 multiply_reduce_fusion.1
  128.8 1.8 convolution_convert_fusion.4
  132.4 3.5 all-to-all-start.2
  136.0 2.7 multiply_convert_fusion.2
  138.7 2.3 convolution_convert_fusion.3
  143.4 16.1 %multiply_reduce_fusion = (f32[6,1024]{1,0:T(8,128)S(1)}, f32[6,1024,1024]{1,2,0:T(8,128)}) fusion(f32[6,1024,1024]{1,2,0:T(8,128)} %get-tuple-element.87, f32[6,1024]{1,0:T(8,128)S(1)} %log_add_fusion, bf16[1024,6,64]{0,2,1:T(8,128)(2,1)S(1)} %reshape.343, bf16[1024,3,6,64]{0,3,2,1:T(8,128)(2,1)} %reshape.337), kind=kOutput, calls=%fused_computation.1 | convolution fusion | flops 824174592 | bytes 51953664 | tf_op jit(solution)/shard_map/while/body/eval_jaxpr/qhd,khd->hqk/dot_general | solution.py:108
  159.6 21.1 %multiply_convert_fusion = bf16[6,1024,1024]{1,2,0:T(8,128)(2,1)} fusion(f32[6,1024,1024]{1,2,0:T(8,128)} %get-tuple-element.92, f32[6,1024,1024]{1,2,0:T(8,128)} %get-tuple-element.87, f32[6,1024]{1,0:T(8,128)S(1)} %get-tuple-element.91, f32[6,1024]{1,0:T(8,128)S(1)} %log_add_fusion), kind=kLoop, calls=%fused_computation | loop fusion | flops 25165824 | bytes 62963712 | tf_op jit(solution)/shard_map/while/body/eval_jaxpr/convert_element_type | solution.py:110
  180.7 10.3 %fusion.43 = bf16[6,64,1024]{2,1,0:T(8,128)(2,1)S(1)} fusion(bf16[1024,6,64]{0,2,1:T(8,128)(2,1)S(1)} %reshape.343, f32[6,1024,1024]{1,2,0:T(8,128)} %get-tuple-element.87, f32[6,1024]{1,0:T(8,128)S(1)} %log_add_fusion), kind=kOutput, calls=%fused_computation.87 | convolution fusion | flops 818282496 | bytes 26763264 | tf_op jit(solution)/shard_map/while/body/eval_jaxpr/hqk,qhd->khd/dot_general | solution.py:111
  191.0 2.9 copy.84
  193.8 8.9 %fusion.65 = f32[6,64,1024]{2,1,0:T(8,128)S(1)} fusion(bf16[1024,6,64]{0,2,1:T(8,128)(2,1)} %copy-done.5, bf16[6,1024,1024]{1,2,0:T(8,128)(2,1)} %multiply_convert_fusion), kind=kOutput, calls=%fused_computation.135 | convolution fusion | flops 805306368 | bytes 14942208 | tf_op jit(solution)/shard_map/while/body/eval_jaxpr/hqk,qhd->khd/dot_general | solution.py:117
  202.7 3.6 bitcast_multiply_fusion.2
  207.5 2.0 fusion.40
  209.5 5.1 copy.83
  214.6 4.8 copy.82
  219.4 6.7 pad_maximum_fusion
  226.1 6.3 all_to_all.61
  232.4 1.7 copy.85
  234.1 4.4 copy.86
  238.5 5.8 convolution_convert_fusion.1
  244.4 6.1 convolution_convert_fusion
  252.3 6.3 fusion.34
  258.6 2.4 all-reduce.3
  261.2 3.0 fusion.33
  264.2 2.1 add_convert_fusion
  266.3 10.6 %reduce-scatter.9.cloned.1.call-done = bf16[384,2304]{1,0:T(8,128)(2,1)} async-done(((bf16[768,2304]{1,0:T(8,128)(2,1)}), bf16[384,2304]{1,0:T(8,128)(2,1)}) %reduce-scatter.9.cloned.1.call-update) | async-done | bytes 1769488 | tf_op jit(solution)/shard_map/reduce_scatter | solution.py:216
  276.9 434.8 %all-reduce.5 = (f32[384]{0:T(512)}, f32[384,2304]{1,0:T(8,128)}, f32[384,768]{1,0:T(8,128)}, f32[384]{0:T(512)}, f32[384,2304]{1,0:T(8,128)}, /*index=5*/f32[576,768]{1,0:T(8,128)}) all-reduce(f32[384]{0:T(512)S(1)} %dynamic-slice_convert_fusion.1, ...), channel_id=1, replica_groups=mesh['dp'=16,'head'=2] {'dp'}, use_global_device_ids=true, to_apply=%region_16.17 | all-reduce | flops 2507520 | bytes 15046656 | tf_op jit(solution)/shard_map/psum | solution.py:223
  (110 shorter events, 17.3 us)
Async XLA Ops:
  7.2 107.7 %copy-start = (bf16[768,2304]{1,0:T(8,128)(2,1)S(1)}, bf16[768,2304]{1,0:T(8,128)(2,1)}, u32[]{:S(2)}) copy-start(bf16[768,2304]{1,0:T(8,128)(2,1)} %param.15) | copy-start | bytes 10616836
  8.7 1.5 copy-start.20
  10.2 0.6 copy-start.22
  25.5 8.1 %all-to-all-start = ((bf16[512,3,2,384]{3,0,1,2:T(8,128)(2,1)}), bf16[512,3,2,384]{3,0,1,2:T(8,128)(2,1)}, u32[]{:S(2)}, u32[]{:S(2)}) async-start(bf16[512,3,2,384]{3,0,1,2:T(8,128)(2,1)} %copy.72), calls=%async_computation | async-start | bytes 4718592 | tf_op jit(solution)/shard_map/all_to_all | solution.py:150
  30.4 235.9 %reduce-scatter.7.cloned.1.call-start = ((), (), s32[]{:S(2)}) async-start(), calls=%async_computation.9 | async-start | bytes 1769472 | tf_op jit(solution)/shard_map/reduce_scatter | solution.py:210
  46.9 3.4 copy-start.26
  53.1 4.2 copy-start.3
  58.0 10.6 %copy-start.4 = (bf16[1024,6,64]{0,2,1:T(8,128)(2,1)}, bf16[1024,6,64]{0,2,1:T(8,128)(2,1)S(1)}, u32[]{:S(2)}) copy-start(bf16[1024,6,64]{0,2,1:T(8,128)(2,1)S(1)} %get-tuple-element.66) | copy-start | bytes 2359300
  58.0 10.6 %copy-start.5 = (bf16[1024,6,64]{0,2,1:T(8,128)(2,1)}, bf16[1024,6,64]{0,2,1:T(8,128)(2,1)S(1)}, u32[]{:S(2)}) copy-start(bf16[1024,6,64]{0,2,1:T(8,128)(2,1)S(1)} %get-tuple-element.67) | copy-start | bytes 2359300
  68.6 10.2 %copy-start.18 = (f32[6,1024]{1,0:T(8,128)}, f32[6,1024]{1,0:T(8,128)S(1)}, u32[]{:S(2)}) copy-start(f32[6,1024]{1,0:T(8,128)S(1)} %get-tuple-element.86) | copy-start | bytes 73732
  78.9 11.4 %copy-start.19 = (f32[6,1024]{1,0:T(8,128)}, f32[6,1024]{1,0:T(8,128)S(1)}, u32[]{:S(2)}) copy-start(f32[6,1024]{1,0:T(8,128)S(1)} %fusion) | copy-start | bytes 73732
  111.9 3.0 copy-start.24
  114.5 13.1 %copy-start.7 = (f32[512,768]{1,0:T(8,128)}, f32[512,768]{1,0:T(8,128)S(1)}, u32[]{:S(2)}) copy-start(f32[512,768]{1,0:T(8,128)S(1)} %get-tuple-element.89) | copy-start | bytes 4718596
  114.9 2.1 copy-start.16
  114.9 2.1 copy-start.27
  117.0 8.2 %copy-start.12 = (f32[512,2304]{1,0:T(8,128)}, f32[512,2304]{1,0:T(8,128)S(1)}, u32[]{:S(2)}) copy-start(f32[512,2304]{1,0:T(8,128)S(1)} %fusion.59) | copy-start | bytes 14155780
  125.2 2.4 copy-start.31
  125.2 2.4 copy-start.32
  127.6 1.1 copy-start.10
  128.8 1.8 copy-start.29
  132.4 9.7 %all-to-all-start.2 = ((bf16[512,2,384]{2,0,1:T(8,128)(2,1)}), bf16[512,2,384]{2,0,1:T(8,128)(2,1)S(1)}, u32[]{:S(2)}, u32[]{:S(2)}) async-start(bf16[512,2,384]{2,0,1:T(8,128)(2,1)} %bitcast.88), calls=%async_computation.2 | async-start | bytes 1572864 | tf_op jit(solution)/shard_map/all_to_all | solution.py:184
  135.9 130.3 %reduce-scatter.11.cloned.1.call-start = ((), (), s32[]{:S(2)}) async-start(), calls=%async_computation.11 | async-start | bytes 2654208 | tf_op jit(solution)/shard_map/reduce_scatter | solution.py:219
  136.0 2.7 copy-start.17
  138.7 2.4 copy-start.13
  141.1 125.2 %reduce-scatter.5.cloned.1.call-start = ((), (), s32[]{:S(2)}) async-start(), calls=%async_computation.8 | async-start | bytes 5308416 | tf_op jit(solution)/shard_map/reduce_scatter | solution.py:207
  193.8 8.9 %copy-start.2 = (bf16[6,1024,1024]{1,2,0:T(8,128)(2,1)S(1)}, bf16[6,1024,1024]{1,2,0:T(8,128)(2,1)}, u32[]{:S(2)}) copy-start(bf16[6,1024,1024]{1,2,0:T(8,128)(2,1)} %multiply_convert_fusion) | copy-start | bytes 37748740
  193.8 8.9 %copy-start.11 = (f32[1024,64]{0,1:T(8,128)S(1)}, f32[1024,64]{0,1:T(8,128)}, u32[]{:S(2)}) copy-start(f32[1024,64]{0,1:T(8,128)} %get-tuple-element.83) | copy-start | bytes 786436
  206.6 1.0 copy-start.15
  209.5 9.9 %copy-start.9 = (bf16[1024,1,1,384]{3,1,2,0:T(2,128)(2,1)S(1)}, bf16[1024,1,1,384]{3,1,2,0:T(2,128)(2,1)}, u32[]{:S(2)}) copy-start(bf16[1024,1,1,384]{3,1,2,0:T(2,128)(2,1)} %copy.84) | copy-start | bytes 2359300
  234.1 4.4 copy-start.6
  234.1 4.4 copy-start.21
  234.1 4.4 copy-start.23
  234.1 4.4 copy-start.25
  244.3 32.6 %reduce-scatter.9.cloned.1.call-start = ((), (), s32[]{:S(2)}) async-start(), calls=%async_computation.10 | async-start | bytes 5308416 | tf_op jit(solution)/shard_map/reduce_scatter | solution.py:216
  250.4 0.7 copy-start.30
  261.2 3.0 copy-start.8
  261.2 3.0 copy-start.14
  261.2 3.0 copy-start.28
  264.2 447.5 %copy-start.1 = (bf16[768,2304]{1,0:T(8,128)(2,1)S(1)}, bf16[768,2304]{1,0:T(8,128)(2,1)}, u32[]{:S(2)}) copy-start(bf16[768,2304]{1,0:T(8,128)(2,1)} %param.15) | copy-start | bytes 10616836
Sparse Core Ops, SparseCore 0:
  130.7 11.1 reduce-scatter.6
  144.8 10.6 reduce-scatter.10
  244.4 16.7 reduce-scatter.4
  263.8 12.9 reduce-scatter.8
where the time goes:
time: 724 us; the launch traced here: 719 us
  blocking collectives  450 us (62%)
  matrix products  107 us (15%)
  other arithmetic  64.2 us (9%)
  local copies, waits for them, and re-layouts  58.7 us (8%)
  between operations  16 us (2%)
  waiting for transfers between devices  13.3 us (2%)
  starting transfers between devices  9.27 us (1%)
    psum x1, blocking collectives, shards(): lax.psum((grad_shares[0], grad_shares[1], grad_shares[2], grad_shares[3],...  435 us
    convert_element_type x1, other arithmetic, slot_backward(): score_change = (probs * (drift - centre)).astype(jnp.bfloat16)  21.1 us
    dot_general x1, matrix products, slot_backward(): jnp.einsum('qhd,khd->hqk', change_out, values, preferred_element_type=jnp...  16.1 us
  transfers between devices with their start and end apart: 6, of which 2 were waited for; matrix products, arithmetic and copies ran while one was open for 17% of the time, Pallas kernels for 0%

commit v1 on v0

--- a/solution.py
+++ b/solution.py
@@ -1,12 +1,16 @@
+import functools
 import math
 
 import jax
 import jax.numpy as jnp
 from jax import lax
+from jax.experimental import pallas as pl
+from jax.experimental.pallas import tpu as pltpu
 from jax.sharding import PartitionSpec as P
 
 HD = 64
 SLOT = 1024
+MESH = pl.DeviceIdType.MESH
 
 
 epsilon = 1e-05
@@ -121,6 +125,312 @@
     key_change = unrotate(key_change, cosine, sine)
     stacked = jnp.stack([query_change, key_change, value_change], axis=1)
     return stacked.astype(jnp.bfloat16).reshape(SLOT, 3, share)
+
+
+def tiles_of(grad):
+    rows, columns = grad.shape
+    half = grad.reshape(2, rows // 32, 16, columns // 128, 128)
+    return half.transpose(0, 3, 1, 2, 4).reshape(2, -1, 16, 128).astype(jnp.bfloat16)
+
+
+def grad_of(tiles, rows, columns):
+    parts = tiles[: rows * columns // 2048].reshape(columns // 128, rows // 16, 16, 128)
+    return parts.transpose(1, 2, 0, 3).reshape(rows, columns).astype(jnp.float32)
+
+
+class Grid:
+    def __init__(self, size):
+        self.a = 2 if size < 64 else 4
+        self.b = size // (self.a * self.a)
+        strides = (1, 32, 4) if size == 128 else (1, self.a, self.a * self.a)
+        dp = lax.axis_index("dp")
+        core = lax.axis_index("head")
+        first = (dp // strides[0]) % self.a
+        second = (dp // strides[1]) % self.a
+        third = (dp // strides[2]) % self.b
+        self.dp, self.core = dp, core
+        self.sizes = (self.a, self.a, self.b)
+        self.place = (
+            first * (1 - core) + second * core,
+            second * (1 - core) + first * core,
+            third,
+        )
+        self.stride = (
+            strides[0] * (1 - core) + strides[1] * core,
+            strides[1] * (1 - core) + strides[0] * core,
+            strides[2],
+        )
+
+    def peer(self, axis, step):
+        index = lax.rem(self.place[axis] + step, self.sizes[axis])
+        return index, (self.dp + (index - self.place[axis]) * self.stride[axis], self.core)
+
+    def barrier(self):
+        sem = pltpu.get_barrier_semaphore()
+        count = 1
+        pl.semaphore_signal(sem, inc=1, device_id=(self.dp, 1 - self.core), device_id_type=MESH)
+        for axis in range(3):
+            for step in range(1, self.sizes[axis]):
+                pl.semaphore_signal(sem, inc=1, device_id=self.peer(axis, step)[1], device_id_type=MESH)
+                count += 1
+        pl.semaphore_wait(sem, count)
+
+
+def sum_into(out_at, terms, length):
+    step = next(n for n in (9, 8, 7, 6, 5, 4, 3, 2, 1) if length % n == 0)
+
+    def body(i, carry):
+        at = i * step
+        value = terms[0](at, step).astype(jnp.float32)
+        for term in terms[1:]:
+            value = value + term(at, step).astype(jnp.float32)
+        out_at(at, step, value.astype(jnp.bfloat16))
+        return carry
+
+    lax.fori_loop(0, length // step, body, 0)
+
+
+def reader(ref, base=0):
+    return lambda at, n: ref[pl.ds(base + at, n)]
+
+
+def writer(ref, base=0):
+    def put(at, n, value):
+        ref[pl.ds(base + at, n)] = value
+
+    return put
+
+
+class Group:
+    def __init__(self, grid, tiles, bufs, sends, recvs):
+        self.grid, self.tiles = grid, tiles
+        self.own, self.got, self.sums, self.whole = bufs
+        self.sends, self.recvs = sends, recvs
+        self.used = 0
+        sizes = grid.sizes
+        self.part = (
+            tiles // sizes[0],
+            tiles // (sizes[0] * sizes[1]),
+            tiles // (sizes[0] * sizes[1] * sizes[2]),
+        )
+        self.flight = []
+
+    def copy(self, source, target, device):
+        slot = self.used
+        self.used += 1
+        copy = pltpu.make_async_remote_copy(
+            src_ref=source,
+            dst_ref=target,
+            send_sem=self.sends.at[slot],
+            recv_sem=self.recvs.at[slot],
+            device_id=device,
+            device_id_type=MESH,
+        )
+        copy.start()
+        self.flight.append(copy)
+
+    def land(self):
+        for copy in self.flight:
+            copy.wait()
+        self.flight = []
+
+    def scatter(self, axis):
+        source = self.own if axis == 0 else self.sums[axis - 1]
+        part = self.part[axis]
+        for step in range(1, self.grid.sizes[axis]):
+            index, device = self.grid.peer(axis, step)
+            self.copy(
+                source.at[pl.ds(index * part, part)], self.got[axis].at[step - 1], device
+            )
+
+    def add(self, axis):
+        self.land()
+        source = self.own if axis == 0 else self.sums[axis - 1]
+        part = self.part[axis]
+        terms = [reader(source, self.grid.place[axis] * part)]
+        for step in range(1, self.grid.sizes[axis]):
+            terms.append(reader(self.got[axis].at[step - 1]))
+        out = writer(self.sums[axis]) if axis < 2 else writer(self.whole, self.offset(2))
+        sum_into(out, terms, part)
+
+    def offset(self, axis):
+        return sum(self.grid.place[k] * self.part[k] for k in range(axis + 1))
+
+    def gather(self, axis):
+        block = self.whole.at[pl.ds(self.offset(axis), self.part[axis])]
+        for step in range(1, self.grid.sizes[axis]):
+            self.copy(block, block, self.grid.peer(axis, step)[1])
+
+    def stages(self):
+        def first():
+            self.scatter(0)
+
+        def turn(axis):
+            def run():
+                self.add(axis)
+                if axis < 2:
+                    self.scatter(axis + 1)
+                else:
+                    self.gather(2)
+
+            return run
+
+        def spread(axis):
+            def run():
+                self.land()
+                self.gather(axis)
+
+            return run
+
+        return [first, turn(0), turn(1), turn(2), spread(1), spread(0), self.land]
+
+
+def group_scratch(tiles, size):
+    a = 2 if size < 64 else 4
+    b = size // (a * a)
+    shape = lambda *s: pltpu.VMEM(s + (16, 128), jnp.bfloat16)
+    copies = 2 * (2 * (a - 1) + (b - 1))
+    return [
+        shape(a - 1, tiles // a),
+        shape(a - 1, tiles // (a * a)),
+        shape(b - 1, tiles // size),
+        shape(tiles // a),
+        shape(tiles // (a * a)),
+        pltpu.SemaphoreType.DMA((copies,)),
+        pltpu.SemaphoreType.DMA((copies,)),
+    ]
+
+
+def reduce_kernel(size, counts, *refs):
+    total = len(counts)
+    ins, refs = refs[:total], refs[total:]
+    vec_in, refs = refs[0], refs[1:]
+    outs, refs = refs[:total], refs[total:]
+    vec_out, refs = refs[0], refs[1:]
+    grid = Grid(size)
+    pair_send, pair_recv, vec_send, vec_recv, vec_got, refs = refs[0], refs[1], refs[2], refs[3], refs[4], refs[5:]
+    owns, refs = refs[:total], refs[total:]
+    theirs, refs = refs[:total], refs[total:]
+    grid.barrier()
+    pair = (grid.dp, 1 - grid.core)
+    copies = []
+    for k in range(total):
+        copy = pltpu.make_async_remote_copy(
+            src_ref=ins[k].at[1 - grid.core],
+            dst_ref=theirs[k],
+            send_sem=pair_send.at[k],
+            recv_sem=pair_recv.at[k],
+            device_id=pair,
+            device_id_type=MESH,
+        )
+        copy.start()
+        copies.append(copy)
+    plans = []
+    for k in range(total):
+        own = refs[7 * k : 7 * k + 7]
+        group = Group(
+            grid, counts[k], (owns[k], own[0:3], own[3:5], outs[k]), own[5], own[6]
+        )
+
+        def join(k=k, group=group):
+            copies[k].wait()
+            sum_into(
+                writer(owns[k]),
+                [reader(ins[k].at[grid.core]), reader(theirs[k])],
+                counts[k],
+            )
+
+        plans.append([join] + group.stages())
+    depth = len(plans[0])
+    for moment in range(depth + total - 1):
+        for k in range(total - 1, -1, -1):
+            if 0 <= moment - k < depth:
+                plans[k][moment - k]()
+    vec_out[...] = vec_in[...]
+    slot = 0
+    legs = [[pair]] + [
+        [grid.peer(axis, step)[1] for step in range(1, grid.sizes[axis])] for axis in range(3)
+    ]
+    for leg in legs:
+        flight = []
+        vec_got[slot, :, :] = vec_out[...]
+        for j, device in enumerate(leg):
+            copy = pltpu.make_async_remote_copy(
+                src_ref=vec_got.at[slot],
+                dst_ref=vec_got.at[slot + 1 + j],
+                send_sem=vec_send.at[slot + j],
+                recv_sem=vec_recv.at[slot + j],
+                device_id=device,
+                device_id_type=MESH,
+            )
+            copy.start()
+            flight.append(copy)
+        for copy in flight:
+            copy.wait()
+        value = vec_got[slot]
+        for j in range(len(leg)):
+            value = value + vec_got[slot + 1 + j]
+        vec_out[...] = value
+        slot += len(leg) + 1
+
+
+def reduce_gradients(mixer_grad, joined_grad, merge_grad, feeder_grad, expand_grad, shrink_grad):
+    size = lax.axis_size("dp")
+    core = lax.axis_index("head")
+
+    def padded(tiles):
+        extra = -tiles.shape[1] % size
+        return jnp.pad(tiles, ((0, 0), (0, extra), (0, 0), (0, 0)))
+
+    ins = [padded(tiles_of(shrink_grad))]
+    for j in range(3):
+        ins.append(padded(tiles_of(expand_grad[:, 768 * j : 768 * j + 768])))
+    ins.append(padded(tiles_of(merge_grad)))
+    for j in range(3):
+        ins.append(padded(tiles_of(joined_grad[:, 768 * j : 768 * j + 768])))
+    counts = [i.shape[1] for i in ins]
+    vec = jnp.concatenate([mixer_grad.reshape(6, 128), feeder_grad.reshape(6, 128), jnp.zeros((4, 128))])
+    vmem = pl.BlockSpec(memory_space=pltpu.VMEM)
+    tile = lambda n: (n, 16, 128)
+    total = len(ins)
+    a = 2 if size < 64 else 4
+    b = size // (a * a)
+    slots = 1 + 2 * (a - 1) + (b - 1) + 4
+    scratch = [
+        pltpu.SemaphoreType.DMA((total,)),
+        pltpu.SemaphoreType.DMA((total,)),
+        pltpu.SemaphoreType.DMA((slots,)),
+        pltpu.SemaphoreType.DMA((slots,)),
+        pltpu.VMEM((slots, 16, 128), jnp.float32),
+    ]
+    scratch += [pltpu.VMEM(tile(n), jnp.bfloat16) for n in counts]
+    scratch += [pltpu.VMEM(tile(n), jnp.bfloat16) for n in counts]
+    for n in counts:
+        scratch += group_scratch(n, size)
+    outs = pl.pallas_call(
+        functools.partial(reduce_kernel, size, counts),
+        out_shape=[jax.ShapeDtypeStruct(tile(n), jnp.bfloat16) for n in counts]
+        + [jax.ShapeDtypeStruct((16, 128), jnp.float32)],
+        in_specs=[vmem] * (total + 1),
+        out_specs=[vmem] * (total + 1),
+        scratch_shapes=scratch,
+        compiler_params=pltpu.CompilerParams(
+            collective_id=0, has_side_effects=True, vmem_limit_bytes=62 << 20
+        ),
+    )(*ins, vec)
+    vec_sum = outs[-1]
+    mixer = lax.dynamic_slice(vec_sum[:6].reshape(768), (core * 384,), (384,))
+    feeder = lax.dynamic_slice(vec_sum[6:12].reshape(768), (core * 384,), (384,))
+    expand = jnp.concatenate([grad_of(outs[j], 384, 768) for j in (1, 2, 3)], axis=1)
+    joined = jnp.concatenate([grad_of(outs[j], 384, 768) for j in (5, 6, 7)], axis=1)
+    return (
+        mixer,
+        joined,
+        grad_of(outs[4], 384, 768),
+        feeder,
+        expand,
+        grad_of(outs[0], 576, 768),
+    )
 
 
 def shards(
@@ -200,47 +510,10 @@
     first_change = jnp.dot(joined_change, joined_weight.T, preferred_element_type=jnp.float32)
     input_part, mixer_grad = normalize_back(first_change, plain_one, factor_one, mixer_gain)
     tokens_gradient = (residual_change + input_part).astype(jnp.bfloat16)
-    grad_shares = (
-        lax.psum_scatter(
-            mixer_grad.astype(jnp.bfloat16), "head", scatter_dimension=0, tiled=True
-        ).astype(jnp.float32),
-        lax.psum_scatter(
-            joined_grad.astype(jnp.bfloat16), "head", scatter_dimension=0, tiled=True
-        ).astype(jnp.float32),
-        lax.psum_scatter(
-            merge_grad.astype(jnp.bfloat16), "head", scatter_dimension=0, tiled=True
-        ).astype(jnp.float32),
-        lax.psum_scatter(
-            feeder_grad.astype(jnp.bfloat16), "head", scatter_dimension=0, tiled=True
-        ).astype(jnp.float32),
-        lax.psum_scatter(
-            expand_grad.astype(jnp.bfloat16), "head", scatter_dimension=0, tiled=True
-        ).astype(jnp.float32),
-        lax.psum_scatter(
-            shrink_grad.astype(jnp.bfloat16), "head", scatter_dimension=0, tiled=True
-        ).astype(jnp.float32),
-    )
-    mixer_total, joined_total, merge_total, feeder_total, expand_total, shrink_total = lax.psum(
-        (
-            grad_shares[0],
-            grad_shares[1],
-            grad_shares[2],
-            grad_shares[3],
-            grad_shares[4],
-            grad_shares[5],
-        ),
-        "dp",
-    )
-    return (
-        block_output,
-        tokens_gradient,
-        mixer_total,
-        joined_total,
-        merge_total,
-        feeder_total,
-        expand_total,
-        shrink_total,
-    )
+    total = reduce_gradients(
+        mixer_grad, joined_grad, merge_grad, feeder_grad, expand_grad, shrink_grad
+    )
+    return (block_output, tokens_gradient) + total
 
 
 def solution(mesh):

time: 724 us -> 428 us (0.59)
  blocking collectives: 450 us -> 4.56 us
  Pallas kernels: 0 us -> 119 us
  local copies, waits for them, and re-layouts: 58.7 us -> 122 us
  between operations: 16 us -> 2.19 us
  waiting for transfers between devices: 13.3 us -> 2.27 us
    psum x1 -> x0, blocking collectives: 435 us -> none  [shards(): lax.psum((grad_shares[0], grad_shares[1], grad_shares[2], grad_shares[3],...]
    pallas_call x0 -> x1, Pallas kernels: none -> 119 us  [reduce_gradients(): pl.pallas_call(functools.partial(reduce_kernel, size, counts), out_shape=...]
    convert_element_type x0 -> x23, local copies, waits for them, and re-layouts: none -> 50.8 us  [the longest x15 46.4 us: tiles_of(): half.transpose(0, 3, 1, 2, 4).reshape(2, -1, 16, 128).astype(jnp.bfloat16)]
    reduce_scatter x4 -> x0, waiting for transfers between devices: 10.6 us -> none  [the longest x1 10.6 us: shards(): lax.psum_scatter(expand_grad.astype(jnp.bfloat16), 'head', scatter_dimens...]
  transfers between devices with their start and end apart: 6 -> 3, of which waited for: 2 -> 2; matrix products, arithmetic and copies ran while one was open for 17% -> 3% of each run, Pallas kernels for 0% -> 0%
where the time goes in v1:
time: 428 us; the launch traced here: 423 us
  local copies, waits for them, and re-layouts  122 us (29%)
  Pallas kernels  119 us (28%)
  matrix products  100 us (23%)
  other arithmetic  58.4 us (14%)
  starting transfers between devices  14.4 us (3%)
  blocking collectives  4.56 us (1%)
    pallas_call x1, Pallas kernels, reduce_gradients(): pl.pallas_call(functools.partial(reduce_kernel, size, counts), out_shape=...  119 us
    convert_element_type x15, local copies, waits for them, and re-layouts, tiles_of(): half.transpose(0, 3, 1, 2, 4).reshape(2, -1, 16, 128).astype(jnp.bfloat16)  46.4 us
    convert_element_type x1, other arithmetic, slot_backward(): score_change = (probs * (drift - centre)).astype(jnp.bfloat16)  16.8 us
    dot_general x1, matrix products, slot_backward(): jnp.einsum('qhd,khd->hqk', change_out, values, preferred_element_type=jnp...  15.9 us
    another operation x3, local copies, waits for them, and re-layouts, slot_backward(): stacked = jnp.stack([query_change, key_change, value_change], axis=1)  12.7 us
    unnamed x100, local copies, waits for them, and re-layouts  12.5 us
    dot_general x1, matrix products, slot_scores(): jnp.einsum('qhd,khd->hqk', queries, keys, preferred_element_type=jnp.floa...  10.6 us
    dot_general x1, matrix products, slot_forward(): jnp.einsum('hqk,khd->qhd', probs, values, preferred_element_type=jnp.floa...  10.5 us
  transfers between devices with their start and end apart: 3, of which 2 were waited for; matrix products, arithmetic and copies ran while one was open for 3% of the time, Pallas kernels for 0%

profile of v1, /device:TPU:0, one launch (start us, length us, event | category | flops | bytes accessed | tf_op | source)
XLA Modules:
  0.0 423.0 jit_solution(2806214956663393977)
XLA Ops:
  4.2 5.8 %convolution_convert_fusion.2 = bf16[512,2304]{1,0:T(8,128)(2,1)} fusion(bf16[768,2304]{1,0:T(8,128)(2,1)} %param.12, bf16[512,768]{1,0:T(8,128)(2,1)} %param.10, f32[768]{0:T(1024)} %param.11, f32[512]{0:T(512)S(1)} %add_rsqrt_fusion.1, f32[512]{0:T(512)S(1)} %broadcast_multiply_fusion.8), kind=kOutput, calls=%fused_computation.13 | convolution fusion | flops 1815085056 | bytes 6691840 | tf_op jit(solution)/shard_map/dot_general | solution.py:457
  10.0 5.6 %reshape.429 = bf16[512,3,2,384]{3,2,1,0:T(2,128)(2,1)} reshape(bf16[512,2304]{1,0:T(8,128)(2,1)} %convolution_convert_fusion.2) | data formatting | bytes 4718592 | tf_op jit(solution)/shard_map/reshape | solution.py:461
  15.6 3.4 copy.221
  18.9 5.2 %all-to-all-start = ((bf16[512,3,2,384]{3,0,1,2:T(8,128)(2,1)}), bf16[512,3,2,384]{3,0,1,2:T(8,128)(2,1)}, u32[]{:S(2)}, u32[]{:S(2)}) async-start(bf16[512,3,2,384]{3,0,1,2:T(8,128)(2,1)} %copy.221), calls=%async_computation | async-start | bytes 4718592 | tf_op jit(solution)/shard_map/all_to_all | solution.py:460
  27.3 6.8 %copy.222 = bf16[2,512,3,1,384]{1,0,4,2,3:T(2,128)(2,1)} copy(bf16[2,512,3,1,384]{4,1,2,0,3:T(8,128)(2,1)} %bitcast.1) | data formatting | bytes 4718592 | tf_op jit(solution)/shard_map/all_to_all | solution.py:460
  34.1 6.6 %reshape.430 = bf16[1024,3,6,64]{0,3,2,1:T(8,128)(2,1)} reshape(bf16[2,512,3,1,384]{1,0,4,2,3:T(2,128)(2,1)} %copy.222) | data formatting | bytes 4718592 | tf_op jit(solution)/shard_map/while/body/eval_jaxpr/reshape | solution.py:82
  46.5 10.6 %fusion.65 = (f32[6,1024]{1,0:T(8,128)S(1)}, f32[6,1024,1024]{1,2,0:T(8,128)}) fusion(bf16[1024,6,64]{0,2,1:T(8,128)(2,1)S(1)} %get-tuple-element.85, bf16[1024,6,64]{0,2,1:T(8,128)(2,1)S(1)} %get-tuple-element.84, pred[1024,1024]{0,1:T(8,128)(4,1)S(1)} %fusion.6), kind=kOutput, calls=%fused_computation.147 | convolution fusion | flops 824174592 | bytes 27811840 | tf_op jit(solution)/shard_map/while/body/eval_jaxpr/qhd,khd->hqk/dot_general | solution.py:85
  57.1 10.2 %fusion = f32[6,1024]{1,0:T(8,128)S(1)} fusion(f32[6,1024,1024]{1,2,0:T(8,128)} %get-tuple-element.107, f32[6,1024]{1,0:T(8,128)S(1)} %get-tuple-element.106), kind=kLoop, calls=%fused_computation.6 | loop fusion | flops 12576768 | bytes 25214976 | tf_op jit(solution)/shard_map/while/body/eval_jaxpr/reduce_sum | solution.py:97
  67.3 10.5 %fusion.47 = bf16[6,64,1024]{2,1,0:T(8,128)(2,1)S(1)} fusion(f32[6,1024,1024]{1,2,0:T(8,128)} %get-tuple-element.107, f32[6,1024]{1,0:T(8,128)S(1)} %fusion, f32[6,1024]{1,0:T(8,128)S(1)} %get-tuple-element.106, bf16[1024,3,6,64]{0,3,2,1:T(8,128)(2,1)S(1)} %copy-done.1), kind=kOutput, calls=%fused_computation.92 | convolution fusion | flops 824573952 | bytes 26804224 | tf_op jit(solution)/shard_map/while/body/eval_jaxpr/hqk,khd->qhd/dot_general | solution.py:99
  80.2 4.6 %all_to_all.60 = bf16[2,2,98304]{2,1,0:T(2,128)(2,1)S(1)} all-to-all(bf16[2,2,98304]{2,1,0:T(2,128)(2,1)S(1)} %reshape.450), channel_id=1, replica_groups=mesh['dp'=16,'head'=2] {'head'}, dimensions={0} | all-to-all | bytes 1572864 | tf_op jit(solution)/shard_map/all_to_all | solution.py:465
  89.1 2.6 fusion.66
  94.2 8.2 %multiply_convert_fusion.1 = (bf16[512,1152]{1,0:T(8,128)(2,1)S(1)}, f32[512,1152]{1,0:T(8,128)}, bf16[512,1152]{1,0:T(8,128)(2,1)S(1)}) fusion(f32[512,2304]{1,0:T(8,128)S(1)} %fusion.59, bf16[512,768]{1,0:T(8,128)(2,1)S(1)} %copy-done.19, bf16[1152,768]{1,0:T(8,128)(2,1)S(1)} %copy-done), kind=kOutput, calls=%fused_computation.32 | convolution fusion | flops 951386112 | bytes 11993088 | tf_op jit(solution)/shard_map/dot_general | solution.py:481
  102.4 2.8 multiply_reduce_fusion.1
  108.6 3.9 all-to-all-start.2
  115.7 10.3 %fusion.44 = bf16[6,64,1024]{2,1,0:T(8,128)(2,1)S(1)} fusion(bf16[1024,6,64]{0,2,1:T(8,128)(2,1)S(1)} %reshape.436, f32[6,1024,1024]{1,2,0:T(8,128)} %get-tuple-element.107, f32[6,1024]{1,0:T(8,128)S(1)} %log_add_fusion), kind=kOutput, calls=%fused_computation.91 | convolution fusion | flops 818282496 | bytes 26763264 | tf_op jit(solution)/shard_map/while/body/eval_jaxpr/hqk,qhd->khd/dot_general | solution.py:115
  126.1 15.9 %multiply_reduce_fusion = (f32[6,1024]{1,0:T(8,128)S(1)}, f32[6,1024,1024]{1,2,0:T(8,128)}) fusion(f32[6,1024,1024]{1,2,0:T(8,128)} %get-tuple-element.107, f32[6,1024]{1,0:T(8,128)S(1)} %log_add_fusion, bf16[1024,6,64]{0,2,1:T(8,128)(2,1)S(1)} %reshape.436, bf16[1024,3,6,64]{0,3,2,1:T(8,128)(2,1)} %reshape.430), kind=kOutput, calls=%fused_computation.1 | convolution fusion | flops 824174592 | bytes 51953664 | tf_op jit(solution)/shard_map/while/body/eval_jaxpr/qhd,khd->hqk/dot_general | solution.py:112
  142.0 2.8 copy.233
  144.8 16.8 %multiply_convert_fusion = bf16[6,1024,1024]{1,2,0:T(8,128)(2,1)S(1)} fusion(f32[6,1024,1024]{1,2,0:T(8,128)} %get-tuple-element.112, f32[6,1024,1024]{1,2,0:T(8,128)} %get-tuple-element.107, f32[6,1024]{1,0:T(8,128)S(1)} %get-tuple-element.111, f32[6,1024]{1,0:T(8,128)S(1)} %log_add_fusion), kind=kLoop, calls=%fused_computation | loop fusion | flops 25165824 | bytes 62963712 | tf_op jit(solution)/shard_map/while/body/eval_jaxpr/convert_element_type | solution.py:114
  161.7 5.1 %fusion.67 = f32[6,64,1024]{2,1,0:T(8,128)S(1)} fusion(bf16[1024,6,64]{0,2,1:T(8,128)(2,1)} %copy-done.3, bf16[6,1024,1024]{1,2,0:T(8,128)(2,1)S(1)} %multiply_convert_fusion), kind=kOutput, calls=%fused_computation.149 | convolution fusion | flops 805306368 | bytes 14942208 | tf_op jit(solution)/shard_map/while/body/eval_jaxpr/hqk,qhd->khd/dot_general | solution.py:121
  166.8 3.5 bitcast_multiply_fusion.2
  173.4 5.1 %copy.232 = bf16[1024,1,1,384]{3,1,2,0:T(2,128)(2,1)} copy(bf16[1024,1,1,384]{0,3,2,1:T(8,128)(2,1)} %bitcast.214) | data formatting | bytes 1572864 | tf_op jit(solution)/shard_map/while/body/eval_jaxpr/stack | solution.py:126
  178.5 4.8 %copy.231 = bf16[1024,1,1,384]{3,1,2,0:T(2,128)(2,1)} copy(bf16[1024,1,1,384]{0,3,2,1:T(8,128)(2,1)} %bitcast.213) | data formatting | bytes 1572864 | tf_op jit(solution)/shard_map/while/body/eval_jaxpr/stack | solution.py:126
  183.3 7.6 %pad_maximum_fusion = bf16[1024,3,1,384]{3,1,2,0:T(4,128)(2,1)} fusion(bf16[1024,1,1,384]{3,1,2,0:T(2,128)(2,1)S(1)} %copy-done.11, bf16[1024,1,1,384]{3,1,2,0:T(2,128)(2,1)} %copy.232, bf16[1024,1,1,384]{3,1,2,0:T(2,128)(2,1)} %copy.231), kind=kLoop, calls=%fused_computation.19 | loop fusion | flops 7077888 | bytes 4718592 | tf_op jit(solution)/shard_map/while/body/eval_jaxpr/stack | solution.py:126
  190.9 5.2 %all-to-all-start.3 = ((bf16[1024,3,1,384]{3,1,2,0:T(4,128)(2,1)}), bf16[1024,3,1,384]{3,1,2,0:T(4,128)(2,1)}, u32[]{:S(2)}, u32[]{:S(2)}) async-start(bf16[1024,3,1,384]{3,1,2,0:T(4,128)(2,1)} %pad_maximum_fusion), calls=%async_computation.3 | async-start | bytes 6291456 | tf_op jit(solution)/shard_map/all_to_all | solution.py:501
  196.2 2.7 multiply_convert_fusion.2
  201.1 2.3 convolution_convert_fusion.3
  203.4 4.0 convolution_convert_fusion.1
  207.5 3.6 copy.234
  211.1 4.5 %copy.235 = bf16[512,3,2,1,384]{0,4,2,1,3:T(8,128)(2,1)} copy(bf16[512,3,2,1,384]{4,0,2,1,3:T(8,128)(2,1)} %bitcast.186) | data formatting | bytes 4718592 | tf_op jit(solution)/shard_map/all_to_all | solution.py:501
  215.7 7.0 %fusion.34 = (f32[768]{0:T(1024)}, f32[512]{0:T(512)S(1)}, f32[512]{0:T(512)}, f32[512,768]{1,0:T(8,128)}) fusion(bf16[512,768]{1,0:T(8,128)(2,1)S(1)} %copy-done.5, f32[512]{0:T(512)S(1)} %copy-done.30, f32[512]{0:T(512)S(1)} %copy-done.28, f32[768]{0:T(1024)S(1)} %copy-done.34, bf16[512,2304]{0,1:T(8,128)(2,1)} %bitcast.215, bf16[768,2304]{1,0:T(8,128)(2,1)} %param.12), kind=kOutput, calls=%fused_computation.64 | convolution fusion | flops 1815476480 | bytes 8271872 | tf_op jit(solution)/shard_map/dot_general | solution.py:510
  222.6 4.1 convolution_convert_fusion
  226.8 4.7 %convert_element_type.276 = bf16[2,36,16,6,128]{4,3,2,1,0:T(8,128)(2,1)} reshape(bf16[1152,768]{1,0:T(8,128)(2,1)} %convolution_convert_fusion.3) | data formatting | bytes 3538944 | tf_op jit(solution)/shard_map/convert_element_type | solution.py:133
  233.4 2.3 copy.240
  235.7 2.3 fusion.43
  241.3 3.8 convert_element_type.285
  245.0 2.6 copy.239
  247.6 3.8 convert_element_type.282
  251.4 2.6 copy.238
  254.0 3.8 convert_element_type.279
  257.7 2.6 copy.237
  260.3 4.0 fusion.61
  264.3 4.0 convert_element_type.297
  268.3 2.6 copy.244
  270.9 3.8 convert_element_type.294
  274.7 2.6 copy.243
  277.3 3.8 convert_element_type.291
  281.1 2.6 copy.242
  286.0 118.6 %shard_map.161 = (bf16[224,16,128]{2,1,0:T(8,128)(2,1)}, bf16[144,16,128]{2,1,0:T(8,128)(2,1)}, bf16[144,16,128]{2,1,0:T(8,128)(2,1)}, bf16[144,16,128]{2,1,0:T(...) custom-call(bf16[2,224,16,128]{3,2,1,0:T(8,128)(2,1)} %pad.4.refs_0_, ...), custom_call_target="tpu_custom_call" | custom-call | tf_op jit(solution)/shard_map/pallas_call | solution.py:410
  (161 shorter events, 58.2 us)
Async XLA Ops:
  0.6 93.5 %copy-start = (bf16[1152,768]{1,0:T(8,128)(2,1)S(1)}, bf16[1152,768]{1,0:T(8,128)(2,1)}, u32[]{:S(2)}) copy-start(bf16[1152,768]{1,0:T(8,128)(2,1)} %param.16) | copy-start | bytes 5308420
  2.1 1.5 copy-start.27
  3.6 0.6 copy-start.29
  18.9 5.9 %copy-start.37 = (s32[1,4]{1,0:T(1,128)S(1)}, s32[1,4]{1,0:T(1,128)}, u32[]{:S(2)}) copy-start(s32[1,4]{1,0:T(1,128)} %param.17) | copy-start | bytes 52
  18.9 8.4 %all-to-all-start = ((bf16[512,3,2,384]{3,0,1,2:T(8,128)(2,1)}), bf16[512,3,2,384]{3,0,1,2:T(8,128)(2,1)}, u32[]{:S(2)}, u32[]{:S(2)}) async-start(bf16[512,3,2,384]{3,0,1,2:T(8,128)(2,1)} %copy.221), calls=%async_computation | async-start | bytes 4718592 | tf_op jit(solution)/shard_map/all_to_all | solution.py:460
  44.1 1.7 copy-start.1
  46.5 10.6 %copy-start.2 = (bf16[1024,6,64]{0,2,1:T(8,128)(2,1)}, bf16[1024,6,64]{0,2,1:T(8,128)(2,1)S(1)}, u32[]{:S(2)}) copy-start(bf16[1024,6,64]{0,2,1:T(8,128)(2,1)S(1)} %get-tuple-element.84) | copy-start | bytes 2359300
  46.5 10.6 %copy-start.3 = (bf16[1024,6,64]{0,2,1:T(8,128)(2,1)}, bf16[1024,6,64]{0,2,1:T(8,128)(2,1)S(1)}, u32[]{:S(2)}) copy-start(bf16[1024,6,64]{0,2,1:T(8,128)(2,1)S(1)} %get-tuple-element.85) | copy-start | bytes 2359300
  86.3 2.8 copy-start.4
  89.1 2.9 copy-start.33
  89.1 2.9 copy-start.38
  91.7 13.6 %copy-start.7 = (f32[512,768]{1,0:T(8,128)}, f32[512,768]{1,0:T(8,128)S(1)}, u32[]{:S(2)}) copy-start(f32[512,768]{1,0:T(8,128)S(1)} %get-tuple-element.109) | copy-start | bytes 4718596
  92.0 2.1 copy-start.19
  94.2 8.2 %copy-start.16 = (f32[512,2304]{1,0:T(8,128)}, f32[512,2304]{1,0:T(8,128)S(1)}, u32[]{:S(2)}) copy-start(f32[512,2304]{1,0:T(8,128)S(1)} %fusion.59) | copy-start | bytes 14155780
  102.4 2.8 copy-start.40
  102.4 2.8 copy-start.42
  105.3 1.5 copy-start.39
  106.8 1.8 copy-start.9
  108.6 5.8 %all-to-all-start.2 = ((bf16[512,2,384]{2,0,1:T(8,128)(2,1)}), bf16[512,2,384]{2,0,1:T(8,128)(2,1)S(1)}, u32[]{:S(2)}, u32[]{:S(2)}) async-start(bf16[512,2,384]{2,0,1:T(8,128)(2,1)} %bitcast.178), calls=%async_computation.2 | async-start | bytes 1572864 | tf_op jit(solution)/shard_map/all_to_all | solution.py:494
  161.7 5.1 %copy-start.13 = (f32[1024,64]{0,1:T(8,128)S(1)}, f32[1024,64]{0,1:T(8,128)}, u32[]{:S(2)}) copy-start(f32[1024,64]{0,1:T(8,128)} %get-tuple-element.101) | copy-start | bytes 786436
  170.5 1.0 copy-start.17
  173.4 9.9 %copy-start.11 = (bf16[1024,1,1,384]{3,1,2,0:T(2,128)(2,1)S(1)}, bf16[1024,1,1,384]{3,1,2,0:T(2,128)(2,1)}, u32[]{:S(2)}) copy-start(bf16[1024,1,1,384]{3,1,2,0:T(2,128)(2,1)} %copy.233) | copy-start | bytes 2359300
  190.9 16.5 %all-to-all-start.3 = ((bf16[1024,3,1,384]{3,1,2,0:T(4,128)(2,1)}), bf16[1024,3,1,384]{3,1,2,0:T(4,128)(2,1)}, u32[]{:S(2)}, u32[]{:S(2)}) async-start(bf16[1024,3,1,384]{3,1,2,0:T(4,128)(2,1)} %pad_maximum_fusion), calls=%async_computation.3 | async-start | bytes 6291456 | tf_op jit(solution)/shard_map/all_to_all | solution.py:501
  196.2 2.8 copy-start.8
  199.0 2.1 copy-start.20
  201.1 2.3 copy-start.41
  201.1 2.3 copy-start.43
  211.1 4.6 %copy-start.5 = (bf16[512,768]{1,0:T(8,128)(2,1)S(1)}, bf16[512,768]{1,0:T(8,128)(2,1)}, u32[]{:S(2)}) copy-start(bf16[512,768]{1,0:T(8,128)(2,1)} %param.10) | copy-start | bytes 2359300
  211.1 4.6 %copy-start.28 = (f32[512]{0:T(512)S(1)}, f32[512]{0:T(512)}, u32[]{:S(2)}) copy-start(f32[512]{0:T(512)} %copy-done.27) | copy-start | bytes 6148
  211.1 4.6 %copy-start.30 = (f32[512]{0:T(512)S(1)}, f32[512]{0:T(512)}, u32[]{:S(2)}) copy-start(f32[512]{0:T(512)} %copy-done.29) | copy-start | bytes 6148
  211.1 4.6 %copy-start.34 = (f32[768]{0:T(1024)S(1)}, f32[768]{0:T(1024)}, u32[]{:S(2)}) copy-start(f32[768]{0:T(1024)} %param.11) | copy-start | bytes 9220
  215.7 7.0 %copy-start.14 = (bf16[512,3,2,1,384]{0,4,2,1,3:T(8,128)(2,1)S(1)}, bf16[512,3,2,1,384]{0,4,2,1,3:T(8,128)(2,1)}, u32[]{:S(2)}) copy-start(bf16[512,3,2,1,384]{0,4,2,1,3:T(8,128)(2,1)} %copy.235) | copy-start | bytes 7077892
  235.7 3.7 copy-start.12
  257.7 2.6 copy-start.36
  283.7 1.6 copy-start.31
  283.7 1.6 copy-start.32
  404.6 3.7 copy-start.26
  408.1 1.1 copy-start.25
  408.6 1.1 copy-start.24
  409.6 1.1 copy-start.23
  410.2 1.1 copy-start.22
  411.1 1.2 copy-start.18
  413.0 1.6 copy-start.21
  414.7 1.7 copy-start.6
  414.7 1.8 copy-start.10
  414.7 2.5 copy-start.15
  414.7 2.5 copy-start.35

commit v2 on v1

--- a/solution.py
+++ b/solution.py
@@ -125,17 +125,6 @@
     key_change = unrotate(key_change, cosine, sine)
     stacked = jnp.stack([query_change, key_change, value_change], axis=1)
     return stacked.astype(jnp.bfloat16).reshape(SLOT, 3, share)
-
-
-def tiles_of(grad):
-    rows, columns = grad.shape
-    half = grad.reshape(2, rows // 32, 16, columns // 128, 128)
-    return half.transpose(0, 3, 1, 2, 4).reshape(2, -1, 16, 128).astype(jnp.bfloat16)
-
-
-def grad_of(tiles, rows, columns):
-    parts = tiles[: rows * columns // 2048].reshape(columns // 128, rows // 16, 16, 128)
-    return parts.transpose(1, 2, 0, 3).reshape(rows, columns).astype(jnp.float32)
 
 
 class Grid:
@@ -301,49 +290,89 @@
     ]
 
 
-def reduce_kernel(size, counts, *refs):
-    total = len(counts)
-    ins, refs = refs[:total], refs[total:]
+def reduce_kernel(size, plan, counts, *refs):
+    total = len(plan)
+    ins, refs = refs[:8], refs[8:]
     vec_in, refs = refs[0], refs[1:]
-    outs, refs = refs[:total], refs[total:]
+    outs, refs = refs[:4], refs[4:]
     vec_out, refs = refs[0], refs[1:]
     grid = Grid(size)
-    pair_send, pair_recv, vec_send, vec_recv, vec_got, refs = refs[0], refs[1], refs[2], refs[3], refs[4], refs[5:]
+    pair_send, pair_recv, vec_send, vec_recv, vec_got, flipped = refs[:6]
+    refs = refs[6:]
     owns, refs = refs[:total], refs[total:]
+    gives, refs = refs[:total], refs[total:]
     theirs, refs = refs[:total], refs[total:]
+    wholes, refs = refs[:total], refs[total:]
     grid.barrier()
     pair = (grid.dp, 1 - grid.core)
-    copies = []
+    plans = []
+    held = [None]
     for k in range(total):
-        copy = pltpu.make_async_remote_copy(
-            src_ref=ins[k].at[1 - grid.core],
-            dst_ref=theirs[k],
-            send_sem=pair_send.at[k],
-            recv_sem=pair_recv.at[k],
-            device_id=pair,
-            device_id_type=MESH,
-        )
-        copy.start()
-        copies.append(copy)
-    plans = []
-    for k in range(total):
+        left, right, column, target = plan[k]
+        rows = ins[left].shape[1] // 2
         own = refs[7 * k : 7 * k + 7]
         group = Group(
-            grid, counts[k], (owns[k], own[0:3], own[3:5], outs[k]), own[5], own[6]
+            grid, counts[k], (owns[k], own[0:3], own[3:5], wholes[k]), own[5], own[6]
         )
 
-        def join(k=k, group=group):
-            copies[k].wait()
-            sum_into(
-                writer(owns[k]),
-                [reader(ins[k].at[grid.core]), reader(theirs[k])],
-                counts[k],
+        def product(half, into, left=left, right=right, column=column, rows=rows):
+            def body(i, carry):
+                at = pl.multiple_of(column + i * 256, 256)
+                block = jnp.dot(
+                    flipped[pl.ds(pl.multiple_of(half * rows, 16), rows), :],
+                    ins[right][:, pl.ds(at, 256)],
+                    preferred_element_type=jnp.float32,
+                ).astype(jnp.bfloat16)
+                for part in range(2):
+                    into[pl.ds((2 * i + part) * (rows // 16), rows // 16)] = block[
+                        :, part * 128 : part * 128 + 128
+                    ].reshape(rows // 16, 16, 128)
+                return carry
+
+            lax.fori_loop(0, 3, body, 0)
+
+        pending = []
+
+        def make(k=k, left=left, product=product, pending=pending, rows=rows):
+            if held[0] != left:
+                flipped[: 2 * rows, :] = ins[left][...].T
+                held[0] = left
+            product(1 - grid.core, gives[k])
+            copy = pltpu.make_async_remote_copy(
+                src_ref=gives[k],
+                dst_ref=theirs[k],
+                send_sem=pair_send.at[k],
+                recv_sem=pair_recv.at[k],
+                device_id=pair,
+                device_id_type=MESH,
             )
-
-        plans.append([join] + group.stages())
+            copy.start()
+            pending.append(copy)
+            product(grid.core, owns[k])
+
+        def join(k=k, group=group, pending=pending):
+            pending[0].wait()
+            used = theirs[k].shape[0]
+            sum_into(writer(owns[k]), [reader(owns[k]), reader(theirs[k])], used)
+            if used < counts[k]:
+                owns[k][used:] = jnp.zeros((counts[k] - used, 16, 128), jnp.bfloat16)
+
+        def finish(k=k, column=column, target=target, rows=rows, group=group):
+            group.land()
+
+            def body(i, carry):
+                block = wholes[k][pl.ds(i * (rows // 16), rows // 16)]
+                outs[target][:, pl.ds(pl.multiple_of(column + i * 128, 128), 128)] = (
+                    block.reshape(rows, 128).astype(jnp.float32)
+                )
+                return carry
+
+            lax.fori_loop(0, 6, body, 0)
+
+        plans.append([make, join] + group.stages()[:-1] + [finish])
     depth = len(plans[0])
     for moment in range(depth + total - 1):
-        for k in range(total - 1, -1, -1):
+        for k in range(total):
             if 0 <= moment - k < depth:
                 plans[k][moment - k]()
     vec_out[...] = vec_in[...]
@@ -374,25 +403,18 @@
         slot += len(leg) + 1
 
 
-def reduce_gradients(mixer_grad, joined_grad, merge_grad, feeder_grad, expand_grad, shrink_grad):
+def reduce_gradients(pairs, mixer_grad, feeder_grad):
     size = lax.axis_size("dp")
     core = lax.axis_index("head")
-
-    def padded(tiles):
-        extra = -tiles.shape[1] % size
-        return jnp.pad(tiles, ((0, 0), (0, extra), (0, 0), (0, 0)))
-
-    ins = [padded(tiles_of(shrink_grad))]
-    for j in range(3):
-        ins.append(padded(tiles_of(expand_grad[:, 768 * j : 768 * j + 768])))
-    ins.append(padded(tiles_of(merge_grad)))
-    for j in range(3):
-        ins.append(padded(tiles_of(joined_grad[:, 768 * j : 768 * j + 768])))
-    counts = [i.shape[1] for i in ins]
+    ins = [array for pair in pairs for array in pair]
+    plan = [(2, 3, 0, 1), (2, 3, 768, 1), (2, 3, 1536, 1), (0, 1, 0, 0), (4, 5, 0, 2)]
+    plan += [(6, 7, 0, 3), (6, 7, 768, 3), (6, 7, 1536, 3)]
+    real = [ins[left].shape[1] // 2 * 768 // 2048 for left, _, _, _ in plan]
+    counts = [n + -n % size for n in real]
     vec = jnp.concatenate([mixer_grad.reshape(6, 128), feeder_grad.reshape(6, 128), jnp.zeros((4, 128))])
     vmem = pl.BlockSpec(memory_space=pltpu.VMEM)
-    tile = lambda n: (n, 16, 128)
-    total = len(ins)
+    tile = lambda n: pltpu.VMEM((n, 16, 128), jnp.bfloat16)
+    total = len(plan)
     a = 2 if size < 64 else 4
     b = size // (a * a)
     slots = 1 + 2 * (a - 1) + (b - 1) + 4
@@ -402,35 +424,30 @@
         pltpu.SemaphoreType.DMA((slots,)),
         pltpu.SemaphoreType.DMA((slots,)),
         pltpu.VMEM((slots, 16, 128), jnp.float32),
+        pltpu.VMEM((max(i.shape[1] for i in ins[::2]), ins[0].shape[0]), jnp.bfloat16),
     ]
-    scratch += [pltpu.VMEM(tile(n), jnp.bfloat16) for n in counts]
-    scratch += [pltpu.VMEM(tile(n), jnp.bfloat16) for n in counts]
+    scratch += [tile(n) for n in counts] + [tile(n) for n in real]
+    scratch += [tile(n) for n in real] + [tile(n) for n in counts]
     for n in counts:
         scratch += group_scratch(n, size)
     outs = pl.pallas_call(
-        functools.partial(reduce_kernel, size, counts),
-        out_shape=[jax.ShapeDtypeStruct(tile(n), jnp.bfloat16) for n in counts]
+        functools.partial(reduce_kernel, size, plan, counts),
+        out_shape=[
+            jax.ShapeDtypeStruct((left.shape[1] // 2, right.shape[1]), jnp.float32)
+            for left, right in pairs
+        ]
         + [jax.ShapeDtypeStruct((16, 128), jnp.float32)],
-        in_specs=[vmem] * (total + 1),
-        out_specs=[vmem] * (total + 1),
+        in_specs=[vmem] * (len(ins) + 1),
+        out_specs=[vmem] * 5,
         scratch_shapes=scratch,
         compiler_params=pltpu.CompilerParams(
-            collective_id=0, has_side_effects=True, vmem_limit_bytes=62 << 20
+            collective_id=0, has_side_effects=True, vmem_limit_bytes=63 << 20
         ),
     )(*ins, vec)
     vec_sum = outs[-1]
     mixer = lax.dynamic_slice(vec_sum[:6].reshape(768), (core * 384,), (384,))
     feeder = lax.dynamic_slice(vec_sum[6:12].reshape(768), (core * 384,), (384,))
-    expand = jnp.concatenate([grad_of(outs[j], 384, 768) for j in (1, 2, 3)], axis=1)
-    joined = jnp.concatenate([grad_of(outs[j], 384, 768) for j in (5, 6, 7)], axis=1)
-    return (
-        mixer,
-        joined,
-        grad_of(outs[4], 384, 768),
-        feeder,
-        expand,
-        grad_of(outs[0], 576, 768),
-    )
+    return (mixer, outs[3], outs[2], feeder, outs[1], outs[0])
 
 
 def shards(
@@ -477,17 +494,14 @@
     block_output = (
         residual + jnp.dot(hidden, shrink_weight, preferred_element_type=jnp.float32)
     ).astype(jnp.bfloat16)
-    shrink_grad = jnp.dot(hidden.T, cotangent, preferred_element_type=jnp.float32)
     hidden_change = jnp.dot(cotangent, shrink_weight.T, preferred_element_type=jnp.float32)
     expand_change = jnp.concatenate(
         [hidden_change * gate * gelu_slope(inner), hidden_change * activated], axis=1
     ).astype(jnp.bfloat16)
-    expand_grad = jnp.dot(second_in.T, expand_change, preferred_element_type=jnp.float32)
     second_change = jnp.dot(expand_change, expand_weight.T, preferred_element_type=jnp.float32)
     residual_part, feeder_grad = normalize_back(second_change, plain_two, factor_two, feeder_gain)
     residual_change = cotangent.astype(jnp.float32) + residual_part
     residual_low = residual_change.astype(jnp.bfloat16)
-    merge_grad = jnp.dot(mixed.T, residual_low, preferred_element_type=jnp.float32)
     mixed_change = jnp.dot(residual_low, merge_weight.T, preferred_element_type=jnp.float32).astype(
         jnp.bfloat16
     )
@@ -506,13 +520,16 @@
         tiled=True,
     )
     joined_change = returned.reshape(rows, 3 * width)
-    joined_grad = jnp.dot(first_in.T, joined_change, preferred_element_type=jnp.float32)
     first_change = jnp.dot(joined_change, joined_weight.T, preferred_element_type=jnp.float32)
     input_part, mixer_grad = normalize_back(first_change, plain_one, factor_one, mixer_gain)
     tokens_gradient = (residual_change + input_part).astype(jnp.bfloat16)
-    total = reduce_gradients(
-        mixer_grad, joined_grad, merge_grad, feeder_grad, expand_grad, shrink_grad
-    )
+    pairs = (
+        (hidden, cotangent),
+        (second_in, expand_change),
+        (mixed, residual_low),
+        (first_in, joined_change),
+    )
+    total = reduce_gradients(pairs, mixer_grad, feeder_grad)
     return (block_output, tokens_gradient) + total
 
 

time: 428 us -> 380 us (0.89)
  local copies, waits for them, and re-layouts: 122 us -> 69 us
  matrix products: 100 us -> 85 us
  Pallas kernels: 119 us -> 129 us
  other arithmetic: 58.4 us -> 65.3 us
    convert_element_type x23 -> x0, local copies, waits for them, and re-layouts: 50.8 us -> none  [the longest x15 46.4 us: tiles_of(): half.transpose(0, 3, 1, 2, 4).reshape(2, -1, 16, 128).astype(jnp.bfloat16)]
    dot_general x4 -> x0, matrix products: 12.8 us -> none  [the longest x1 4.13 us: shards(): jnp.dot(first_in.T, joined_change, preferred_element_type=jnp.float32)]
    pallas_call x1, Pallas kernels: 119 us -> 129 us  [reduce_gradients(): pl.pallas_call(functools.partial(reduce_kernel, size, plan, counts), out_...]
    unnamed x100 -> x77, local copies, waits for them, and re-layouts: 12.5 us -> 22.2 us
    slice x3 -> x0, local copies, waits for them, and re-layouts: 6.03 us -> none  [the longest x1 3.96 us: reduce_gradients(): ins.append(padded(tiles_of(joined_grad[:, 768 * j:768 * j + 768])))]
    all_to_all x2, local copies, waits for them, and re-layouts: 8.16 us -> 2.75 us  [shards(): lax.all_to_all(head_changes.reshape(rows * group, 3, 1, share), 'head', s...]
  transfers between devices with their start and end apart: 3 -> 3, of which waited for: 2 -> 2; matrix products, arithmetic and copies ran while one was open for 3% -> 2% of each run, Pallas kernels for 0% -> 0%
where the time goes in v2:
time: 380 us; the launch traced here: 375 us
  Pallas kernels  129 us (34%)
  matrix products  85 us (22%)
  local copies, waits for them, and re-layouts  69 us (18%)
  other arithmetic  65.3 us (17%)
  starting transfers between devices  12.6 us (3%)
  blocking collectives  6.88 us (2%)
  waiting for transfers between devices  5.02 us (1%)
    pallas_call x1, Pallas kernels, reduce_gradients(): pl.pallas_call(functools.partial(reduce_kernel, size, plan, counts), out_...  129 us
    unnamed x77, local copies, waits for them, and re-layouts  22.2 us
    convert_element_type x1, other arithmetic, slot_backward(): score_change = (probs * (drift - centre)).astype(jnp.bfloat16)  17.1 us
    dot_general x1, matrix products, slot_backward(): jnp.einsum('qhd,khd->hqk', change_out, values, preferred_element_type=jnp...  15.6 us
    another operation x3, local copies, waits for them, and re-layouts, slot_backward(): stacked = jnp.stack([query_change, key_change, value_change], axis=1)  13.9 us
    dot_general x1, matrix products, slot_backward(): jnp.einsum('hqk,qhd->khd', probs.astype(jnp.bfloat16), change_out, prefer...  13.2 us
    dot_general x1, matrix products, slot_forward(): jnp.einsum('hqk,khd->qhd', probs, values, preferred_element_type=jnp.floa...  11.4 us
    dot_general x1, matrix products, slot_scores(): jnp.einsum('qhd,khd->hqk', queries, keys, preferred_element_type=jnp.floa...  10.6 us
  transfers between devices with their start and end apart: 3, of which 2 were waited for; matrix products, arithmetic and copies ran while one was open for 2% of the time, Pallas kernels for 0%

profile of v2, /device:TPU:0, one launch (start us, length us, event | category | flops | bytes accessed | tf_op | source)
XLA Modules:
  0.0 375.2 jit_solution(16478580264123587984)
XLA Ops:
  6.4 5.4 %convolution_convert_fusion = bf16[512,2304]{1,0:T(8,128)(2,1)} fusion(bf16[512,768]{1,0:T(8,128)(2,1)S(1)} %fusion.28.refs_6_, bf16[768,2304]{1,0:T(8,128)(2,1)} %param.12), kind=kOutput, calls=%fused_computation.11 | convolution fusion | flops 1813118976 | bytes 6684672 | tf_op jit(solution)/shard_map/dot_general | solution.py:474
  11.8 4.6 %reshape.348 = bf16[512,3,2,384]{3,2,1,0:T(2,128)(2,1)S(1)} reshape(bf16[512,2304]{1,0:T(8,128)(2,1)} %convolution_convert_fusion) | data formatting | bytes 4718592 | tf_op jit(solution)/shard_map/reshape | solution.py:478
  16.4 1.7 copy.66
  18.1 4.1 %all-to-all-start = ((bf16[512,3,2,384]{3,0,1,2:T(8,128)(2,1)}), bf16[512,3,2,384]{3,0,1,2:T(8,128)(2,1)S(1)}, u32[]{:S(2)}, u32[]{:S(2)}) async-start(bf16[512,3,2,384]{3,0,1,2:T(8,128)(2,1)} %copy.66), calls=%async_computation | async-start | bytes 4718592 | tf_op jit(solution)/shard_map/all_to_all | solution.py:477
  22.3 3.0 all-to-all-done
  25.3 4.6 %copy.67 = bf16[2,512,3,1,384]{1,0,4,2,3:T(2,128)(2,1)} copy(bf16[2,512,3,1,384]{4,1,2,0,3:T(8,128)(2,1)S(1)} %bitcast.97) | data formatting | bytes 4718592 | tf_op jit(solution)/shard_map/all_to_all | solution.py:477
  29.9 5.5 %reshape.349 = bf16[1024,3,6,64]{0,3,2,1:T(8,128)(2,1)S(1)} reshape(bf16[2,512,3,1,384]{1,0,4,2,3:T(2,128)(2,1)} %copy.67) | data formatting | bytes 4718592 | tf_op jit(solution)/shard_map/while/body/eval_jaxpr/reshape | solution.py:82
  35.5 2.1 fusion.46
  37.9 1.7 broadcast_multiply_fusion.1
  40.3 2.3 slice_negate_fusion.2
  44.9 10.6 %fusion.57 = (f32[6,1024]{1,0:T(8,128)S(1)}, f32[6,1024,1024]{1,2,0:T(8,128)}) fusion(bf16[1024,6,64]{0,2,1:T(8,128)(2,1)S(1)} %get-tuple-element.71, bf16[1024,6,64]{0,2,1:T(8,128)(2,1)S(1)} %get-tuple-element.70, pred[1024,1024]{0,1:T(8,128)(4,1)S(1)} %fusion.6), kind=kOutput, calls=%fused_computation.126 | convolution fusion | flops 824174592 | bytes 27811840 | tf_op jit(solution)/shard_map/while/body/eval_jaxpr/qhd,khd->hqk/dot_general | solution.py:85
  55.5 10.2 %fusion = f32[6,1024]{1,0:T(8,128)S(1)} fusion(f32[6,1024,1024]{1,2,0:T(8,128)} %get-tuple-element.93, f32[6,1024]{1,0:T(8,128)S(1)} %get-tuple-element.92), kind=kLoop, calls=%fused_computation.6 | loop fusion | flops 12576768 | bytes 25214976 | tf_op jit(solution)/shard_map/while/body/eval_jaxpr/reduce_sum | solution.py:97
  65.7 11.4 %fusion.45 = bf16[6,64,1024]{2,1,0:T(8,128)(2,1)} fusion(f32[6,1024,1024]{1,2,0:T(8,128)} %get-tuple-element.93, f32[6,1024]{1,0:T(8,128)S(1)} %fusion, f32[6,1024]{1,0:T(8,128)S(1)} %get-tuple-element.92, bf16[1024,3,6,64]{0,3,2,1:T(8,128)(2,1)S(1)} %reshape.349), kind=kOutput, calls=%fused_computation.83 | convolution fusion | flops 824573952 | bytes 26804224 | tf_op jit(solution)/shard_map/while/body/eval_jaxpr/hqk,khd->qhd/dot_general | solution.py:99
  77.6 3.0 reduce
  80.6 2.3 copy.90
  82.9 2.0 reshape.363
  84.9 6.9 %all_to_all.60 = bf16[2,2,98304]{2,1,0:T(2,128)(2,1)} all-to-all(bf16[2,2,98304]{2,1,0:T(2,128)(2,1)} %reshape.363), channel_id=1, replica_groups=mesh['dp'=16,'head'=2] {'head'}, dimensions={0} | all-to-all | bytes 1572864 | tf_op jit(solution)/shard_map/all_to_all | solution.py:482
  91.7 2.6 reshape.364
  94.3 1.7 copy.85
  100.7 2.0 fusion.59
  102.8 8.2 %multiply_convert_fusion.1 = (bf16[512,1152]{1,0:T(8,128)(2,1)S(1)}, f32[512,1152]{1,0:T(8,128)}, bf16[512,1152]{1,0:T(8,128)(2,1)S(1)}) fusion(f32[512,2304]{1,0:T(8,128)S(1)} %fusion.59, bf16[512,768]{1,0:T(8,128)(2,1)S(1)} %copy-done.13, bf16[1152,768]{1,0:T(8,128)(2,1)S(1)} %copy-done.31), kind=kOutput, calls=%fused_computation.29 | convolution fusion | flops 951386112 | bytes 11993088 | tf_op jit(solution)/shard_map/dot_general | solution.py:497
  111.0 2.3 multiply_reduce_fusion.1
  113.4 1.7 fusion.53
  116.9 4.5 %all-to-all-start.2 = ((bf16[512,2,384]{2,0,1:T(8,128)(2,1)}), bf16[512,2,384]{2,0,1:T(8,128)(2,1)}, u32[]{:S(2)}, u32[]{:S(2)}) async-start(bf16[512,2,384]{2,0,1:T(8,128)(2,1)} %bitcast.100), calls=%async_computation.2 | async-start | bytes 1572864 | tf_op jit(solution)/shard_map/all_to_all | solution.py:508
  121.5 2.0 all-to-all-done.2
  123.5 3.0 copy.72
  126.5 3.2 reshape.355
  129.7 13.2 %fusion.42 = bf16[6,64,1024]{2,1,0:T(8,128)(2,1)} fusion(bf16[1024,6,64]{0,2,1:T(8,128)(2,1)} %reshape.355, f32[6,1024,1024]{1,2,0:T(8,128)} %get-tuple-element.93, f32[6,1024]{1,0:T(8,128)S(1)} %log_add_fusion), kind=kOutput, calls=%fused_computation.82 | convolution fusion | flops 818282496 | bytes 26763264 | tf_op jit(solution)/shard_map/while/body/eval_jaxpr/hqk,qhd->khd/dot_general | solution.py:115
  143.0 15.6 %multiply_reduce_fusion = (f32[6,1024]{1,0:T(8,128)S(1)}, f32[6,1024,1024]{1,2,0:T(8,128)}) fusion(f32[6,1024,1024]{1,2,0:T(8,128)} %get-tuple-element.93, f32[6,1024]{1,0:T(8,128)S(1)} %log_add_fusion, bf16[1024,6,64]{0,2,1:T(8,128)(2,1)} %reshape.355, bf16[1024,3,6,64]{0,3,2,1:T(8,128)(2,1)S(1)} %reshape.349), kind=kOutput, calls=%fused_computation.1 | convolution fusion | flops 824174592 | bytes 51961856 | tf_op jit(solution)/shard_map/while/body/eval_jaxpr/qhd,khd->hqk/dot_general | solution.py:112
  158.5 4.8 %copy.78 = bf16[1024,1,1,384]{3,1,2,0:T(2,128)(2,1)} copy(bf16[1024,1,1,384]{0,3,2,1:T(8,128)(2,1)} %bitcast.99) | data formatting | bytes 1572864 | tf_op jit(solution)/shard_map/while/body/eval_jaxpr/stack | solution.py:126
  163.3 17.1 %multiply_convert_fusion = bf16[6,1024,1024]{1,2,0:T(8,128)(2,1)S(1)} fusion(f32[6,1024,1024]{1,2,0:T(8,128)} %get-tuple-element.98, f32[6,1024,1024]{1,2,0:T(8,128)} %get-tuple-element.93, f32[6,1024]{1,0:T(8,128)S(1)} %get-tuple-element.97, f32[6,1024]{1,0:T(8,128)S(1)} %log_add_fusion), kind=kLoop, calls=%fused_computation | loop fusion | flops 25165824 | bytes 62963712 | tf_op jit(solution)/shard_map/while/body/eval_jaxpr/convert_element_type | solution.py:114
  180.4 3.9 %fusion.60 = f32[6,64,1024]{2,1,0:T(8,128)S(1)} fusion(bf16[1024,6,64]{0,2,1:T(8,128)(2,1)S(1)} %copy-done.5, bf16[6,1024,1024]{1,2,0:T(8,128)(2,1)S(1)} %multiply_convert_fusion), kind=kOutput, calls=%fused_computation.129 | convolution fusion | flops 805306368 | bytes 14942208 | tf_op jit(solution)/shard_map/while/body/eval_jaxpr/hqk,qhd->khd/dot_general | solution.py:121
  184.3 2.5 bitcast_multiply_fusion.2
  188.0 2.0 fusion.40
  189.9 4.3 %copy.77 = bf16[1024,1,1,384]{3,1,2,0:T(2,128)(2,1)S(1)} copy(bf16[1024,1,1,384]{0,3,2,1:T(8,128)(2,1)} %bitcast.106) | data formatting | bytes 1572864 | tf_op jit(solution)/shard_map/while/body/eval_jaxpr/stack | solution.py:126
  194.2 4.8 %copy.76 = bf16[1024,1,1,384]{3,1,2,0:T(2,128)(2,1)} copy(bf16[1024,1,1,384]{0,3,2,1:T(8,128)(2,1)} %bitcast.105) | data formatting | bytes 1572864 | tf_op jit(solution)/shard_map/while/body/eval_jaxpr/stack | solution.py:126
  199.1 7.7 %pad_maximum_fusion = bf16[1024,3,1,384]{3,1,2,0:T(4,128)(2,1)} fusion(bf16[1024,1,1,384]{3,1,2,0:T(2,128)(2,1)S(1)} %copy-done.6, bf16[1024,1,1,384]{3,1,2,0:T(2,128)(2,1)S(1)} %copy.77, bf16[1024,1,1,384]{3,1,2,0:T(2,128)(2,1)} %copy.76), kind=kLoop, calls=%fused_computation.16 | loop fusion | flops 7077888 | bytes 4718592 | tf_op jit(solution)/shard_map/while/body/eval_jaxpr/stack | solution.py:126
  206.8 3.9 %all-to-all-start.3 = ((bf16[1024,3,1,384]{3,1,2,0:T(4,128)(2,1)}), bf16[1024,3,1,384]{3,1,2,0:T(4,128)(2,1)S(1)}, u32[]{:S(2)}, u32[]{:S(2)}) async-start(bf16[1024,3,1,384]{3,1,2,0:T(4,128)(2,1)} %pad_maximum_fusion), calls=%async_computation.3 | async-start | bytes 6291456 | tf_op jit(solution)/shard_map/all_to_all | solution.py:515
  210.8 3.4 pad_maximum_fusion.1.refs_3_
  214.2 2.0 multiply_convert_fusion.2.refs_0_
  217.2 2.1 add_convert_fusion
  219.7 2.4 copy.80
  222.1 3.0 reshape.356.refs_7_
  225.2 6.0 %fusion.34 = (f32[768]{0:T(1024)S(1)}, f32[512]{0:T(512)S(1)}, f32[512]{0:T(512)S(1)}, f32[512,768]{1,0:T(8,128)}) fusion(bf16[512,768]{1,0:T(8,128)(2,1)S(1)} %copy-done.3, f32[512]{0:T(512)S(1)} %copy-done.26, f32[512]{0:T(512)S(1)} %copy-done.24, f32[768]{0:T(1024)S(1)} %copy-done.28, bf16[512,2304]{1,0:T(8,128)(2,1)} %reshape.356.refs_7_, ...), kind=kOutput, calls=%fused_computation.58 | convolution fusion | flops 1815476480 | bytes 8271872 | tf_op jit(solution)/shard_map/dot_general | solution.py:523
  232.0 129.3 %shard_map.161 = (f32[576,768]{1,0:T(8,128)}, f32[384,2304]{1,0:T(8,128)}, f32[384,768]{1,0:T(8,128)}, f32[384,2304]{1,0:T(8,128)}, f32[16,128]{1,0:T(8,128)}) custom-call(bf16[512,1152]{1,0:T(8,128)(2,1)} %copy-done.7, bf16[512,768]{1,0:T(8,128)(2,1)} %refs_1_.1, bf16[512,768]{1,0:T(8,128)(2,1)} %copy-done.12, bf16[512,2304]{1,0:T(8,128)(2,1)} %pad_maximum_fusion.1.refs_3_, ...), custom_call_target="tpu_custom_call" | custom-call | tf_op jit(solution)/shard_map/pallas_call | solution.py:433
  363.4 3.5 fusion.33
  366.9 1.8 copy.96
  370.9 1.8 copy.98
  (108 shorter events, 25.1 us)
Async XLA Ops:
  2.0 1.5 copy-start.23
  3.5 0.6 copy-start.25
  5.5 0.9 copy-start.10
  18.1 7.1 %all-to-all-start = ((bf16[512,3,2,384]{3,0,1,2:T(8,128)(2,1)}), bf16[512,3,2,384]{3,0,1,2:T(8,128)(2,1)S(1)}, u32[]{:S(2)}, u32[]{:S(2)}) async-start(bf16[512,3,2,384]{3,0,1,2:T(8,128)(2,1)} %copy.66), calls=%async_computation | async-start | bytes 4718592 | tf_op jit(solution)/shard_map/all_to_all | solution.py:477
  35.4 2.1 copy-start.29
  44.9 10.6 %copy-start.4 = (bf16[1024,6,64]{0,2,1:T(8,128)(2,1)}, bf16[1024,6,64]{0,2,1:T(8,128)(2,1)S(1)}, u32[]{:S(2)}) copy-start(bf16[1024,6,64]{0,2,1:T(8,128)(2,1)S(1)} %get-tuple-element.71) | copy-start | bytes 2359300
  94.3 2.6 copy-start.2
  94.3 2.6 copy-start.33
  96.9 1.3 copy-start.11
  97.0 1.2 copy-start.27
  97.9 15.5 %copy-start = (f32[512,768]{1,0:T(8,128)}, f32[512,768]{1,0:T(8,128)S(1)}, u32[]{:S(2)}) copy-start(f32[512,768]{1,0:T(8,128)S(1)} %get-tuple-element.95) | copy-start | bytes 4718596
  97.9 2.9 copy-start.30
  98.5 0.9 copy-start.12
  100.7 2.0 copy-start.13
  100.7 2.0 copy-start.31
  102.8 8.2 %copy-start.19 = (f32[512,2304]{1,0:T(8,128)}, f32[512,2304]{1,0:T(8,128)S(1)}, u32[]{:S(2)}) copy-start(f32[512,2304]{1,0:T(8,128)S(1)} %fusion.59) | copy-start | bytes 14155780
  111.0 2.3 copy-start.20
  111.0 2.3 copy-start.21
  115.1 1.8 copy-start.14
  116.9 6.6 %all-to-all-start.2 = ((bf16[512,2,384]{2,0,1:T(8,128)(2,1)}), bf16[512,2,384]{2,0,1:T(8,128)(2,1)}, u32[]{:S(2)}, u32[]{:S(2)}) async-start(bf16[512,2,384]{2,0,1:T(8,128)(2,1)} %bitcast.100), calls=%async_computation.2 | async-start | bytes 1572864 | tf_op jit(solution)/shard_map/all_to_all | solution.py:508
  163.3 17.1 %copy-start.5 = (bf16[1024,6,64]{0,2,1:T(8,128)(2,1)S(1)}, bf16[1024,6,64]{0,2,1:T(8,128)(2,1)}, u32[]{:S(2)}) copy-start(bf16[1024,6,64]{0,2,1:T(8,128)(2,1)} %copy-done.4) | copy-start | bytes 2359300
  180.4 3.9 %copy-start.15 = (f32[1024,64]{0,1:T(8,128)S(1)}, f32[1024,64]{0,1:T(8,128)}, u32[]{:S(2)}) copy-start(f32[1024,64]{0,1:T(8,128)} %get-tuple-element.87) | copy-start | bytes 786436
  187.0 1.0 copy-start.22
  189.9 9.1 %copy-start.6 = (bf16[1024,1,1,384]{3,1,2,0:T(2,128)(2,1)S(1)}, bf16[1024,1,1,384]{3,1,2,0:T(2,128)(2,1)}, u32[]{:S(2)}) copy-start(bf16[1024,1,1,384]{3,1,2,0:T(2,128)(2,1)} %copy.78) | copy-start | bytes 2359300
  206.8 12.5 %all-to-all-start.3 = ((bf16[1024,3,1,384]{3,1,2,0:T(4,128)(2,1)}), bf16[1024,3,1,384]{3,1,2,0:T(4,128)(2,1)S(1)}, u32[]{:S(2)}, u32[]{:S(2)}) async-start(bf16[1024,3,1,384]{3,1,2,0:T(4,128)(2,1)} %pad_maximum_fusion), calls=%async_computation.3 | async-start | bytes 6291456 | tf_op jit(solution)/shard_map/all_to_all | solution.py:515
  210.8 3.4 copy-start.16
  214.2 3.1 copy-start.1
  214.2 3.1 copy-start.32
  216.2 1.0 copy-start.7
  222.1 3.1 copy-start.3
  222.1 3.1 copy-start.24
  222.1 3.1 copy-start.26
  222.1 3.1 copy-start.28
  363.4 3.5 copy-start.9
  366.9 2.1 copy-start.18
  366.9 4.1 %copy-start.8 = (f32[384,2304]{1,0:T(8,128)S(1)}, f32[384,2304]{1,0:T(8,128)}, u32[]{:S(2)}) copy-start(f32[384,2304]{1,0:T(8,128)} %get-tuple-element.117) | copy-start | bytes 10616836
  370.9 2.8 copy-start.17
